TPU v7x, 32 devices: a whole 2x2x4 slice. The times are simulated.
32 devices in a mesh: grp: 4 (over x, core), dev: 8 (over z, y).
Axes of the slice: x: 2, y: 2, z: 4, core: 2. Of those that a mesh axis runs over, the one named last changes fastest.
Arguments:
- layer_input: bfloat16 [65536, 1024], P(('grp', 'dev')), may hold values from -6 to 6
- hidden_pre: bfloat16 [65536, 1024], P(('grp', 'dev')), may hold values from -6 to 6
- out_grad: bfloat16 [65536, 512], P(('grp', 'dev')), may hold values from -6 to 6
- second_weight: bfloat16 [1024, 512], replicated, may hold values from -0.25 to 0.25
- row_grads: bfloat16 [16384, 128], P(('grp', 'dev')), may hold values from -6 to 6
- row_ids: int32 [16384], P(('grp', 'dev')), may hold values from 0 to 2047
- block_counts: int32 [256], P(('grp', 'dev')), may hold values from 1 to 64, as said below
- emb_table: float32 [16384, 128], P('dev'), may hold values from -4 to 4
- adagrad_state: float32 [16384, 128], P('dev'), may hold values from 0.01 to 1
Outputs:
- grad_first: float32 [1024, 1024], P(('grp', 'dev'))
- grad_second: float32 [1024, 512], P(('grp', 'dev'))
- new_table: float32 [16384, 128], P('dev')
- new_state: float32 [16384, 128], P('dev')
Inputs may be any that keep to these rules, and one draw needn't show every extreme that they name: `block_counts`: the used slots of a block are its first ones. In every draw some owner receives full blocks of 64 used slots from every device. `row_ids`: only used slots are read.
All inputs are finite; a program needn't handle non-finite values.
Results may differ from a plain program's by a relative error of at most 0.0029.
Values may be sent and summed in bfloat16 or wider, within the bound.
A program may use at most 128 MiB of HBM per device.

v0:
```python
import functools

import jax
import jax.numpy as jnp
from jax import lax
from jax.experimental import pallas as pl
from jax.experimental.pallas import tpu as pltpu
from jax.sharding import PartitionSpec as P

learn_rate = 0.5
epsilon = 1e-08
MESH = pl.DeviceIdType.MESH
LANES = 128


def kernel(
    G, D,
    x_hbm, h_hbm, og_hbm, w2_hbm, rg_hbm, ids_hbm,
    g1_ref, g2_ref, tg_hbm,
    x_v, h_v, og_v, w2_v, wt_v, tg_v, dh_v, lt_v,
    eb, ib,
    cs2, cr2, xs2, xr2, kp2, zs2, zf2, zr2,
    cs1, cr1, xs1, xr1, kp1, zs1, zf1, zr1,
    lsem, cs_s, cr_s, xs_s, xr_s, zs_s, zr_s, e1s, e1r, e2s, e2r,
):
    GX, DH = G // 2, D // 2
    g, d = lax.axis_index("grp"), lax.axis_index("dev")
    gx, c = g // 2, g % 2
    dh, dl = d // 2, d % 2
    tokens = x_v.shape[0]
    R = g1_ref.shape[0]
    DR = D * R
    tile = 256
    wide = min(tokens, 1024)
    f32, bf16 = jnp.float32, jnp.bfloat16

    def local(src, dst, i):
        return pltpu.make_async_copy(src, dst, lsem.at[i])

    loads = [
        local(w2_hbm, w2_v, 0),
        local(h_hbm, h_v, 1),
        local(og_hbm, og_v, 2),
        local(x_hbm, x_v, 3),
        local(rg_hbm.at[d], eb.at[g, d], 4),
        local(ids_hbm.at[d], ib.at[g, d], 5),
    ]
    for load in loads:
        load.start()

    peers = [(gx * 2 + (c + 1) % 2, d)]
    plane = []
    for kx in range(GX):
        for kl in range(2):
            if kx or kl:
                plane.append((kx, kl, ((gx + kx) % GX) * 2 + c, dh * 2 + (dl + kl) % 2))
    line = [(k, ((dh + k) % DH) * 2 + dl) for k in range(1, DH)]
    owners = [(k, (d + k) % D) for k in range(1, D)]
    groups = [(k, (g + k) % G) for k in range(1, G)]
    for kx, kl, pg, pd in plane:
        peers.append((pg, pd))
    for k, pd in owners:
        peers.append((g, pd))
    for k, pg in groups:
        peers.append((pg, d))
    barrier = pltpu.get_barrier_semaphore()
    for peer in peers:
        pl.semaphore_signal(barrier, inc=1, device_id=peer, device_id_type=MESH)
    pl.semaphore_wait(barrier, len(peers))

    def remote(src, dst, ss, rs, to):
        return pltpu.make_async_remote_copy(
            src_ref=src, dst_ref=dst, send_sem=ss, recv_sem=rs, device_id=to, device_id_type=MESH
        )

    pending = []

    def send(*args):
        copy = remote(*args)
        copy.start()
        pending.append(copy)

    for k, pd in owners:
        send(rg_hbm.at[pd], eb.at[g, d], e1s.at[0, k], e1r.at[0, k], (g, pd))
        send(ids_hbm.at[pd], ib.at[g, d], e1s.at[1, k], e1r.at[1, k], (g, pd))

    other = (gx * 2 + (c + 1) % 2, d)

    def transpose(src, target_group, relu):
        cols = pl.ds(pl.multiple_of(target_group * DR, DR), DR)

        for t in range(0, tokens, wide):
            block = src[t : t + wide, cols]
            if relu:
                block = jnp.maximum(block, jnp.zeros_like(block))
            lt_v[:, t : t + wide] = block.T

    def product(rhs, out_tile):
        width = rhs.shape[1]

        def body(n, _):
            ns = pl.ds(pl.multiple_of(n * tile, tile), tile)
            out_tile(ns, jnp.dot(lt_v[...], rhs[:, ns], preferred_element_type=f32))
            return 0

        lax.fori_loop(0, width // tile, body, 0)

    order = [1 % GX] + [k for k in range(GX) if k != 1 % GX]

    def away(only, a, src, relu, rhs, cs, cr):
        for kx in (only,):
            transpose(src, ((gx + kx) % GX) * 2 + (c + 1) % 2, relu)

            def put(ns, value, kx=kx):
                cs[kx, :, ns] = value

            product(rhs, put)
            send(cs.at[kx], cr.at[kx], cs_s.at[a, kx], cr_s.at[a, kx], other)

    def home(only, a, src, relu, rhs, cr, xs, xr, kp):
        for kx in (only,):
            transpose(src, ((gx + kx) % GX) * 2 + c, relu)
            remote(cr.at[kx], cr.at[kx], cs_s.at[a, kx], cr_s.at[a, kx], other).wait_recv()

            def put(ns, value, kx=kx):
                value = value + cr[kx, :, ns]
                for b in range(DH):
                    for l in range(2):
                        at = (b * 2 + l) * R
                        piece = value[at : at + R]
                        xs[kx, l, b, :, ns] = piece.astype(bf16)
                        if kx == 0:
                            kp[l, b, :, ns] = piece

            product(rhs, put)
            for px, kl, pg, pd in plane[::-1]:
                if px == kx:
                    i = px * 2 + kl
                    send(xs.at[kx, (dl + kl) % 2], xr.at[i], xs_s.at[a, i], xr_s.at[a, i], (pg, pd))

    def along(a, xr, kp, zs, zf, zr):
        for px, kl, pg, pd in plane:
            i = px * 2 + kl
            remote(xr.at[i], xr.at[i], xs_s.at[a, i], xr_s.at[a, i], (pg, pd)).wait_recv()
        for b in range(DH):
            value = kp[dl, b]
            for px, kl, pg, pd in plane:
                value = value + xr[px * 2 + kl, b].astype(f32)
            zf[b] = value
            zs[b] = value.astype(bf16)
        for k, pd in line[::-1]:
            send(zs.at[(dh + k) % DH], zr.at[k], zs_s.at[a, k], zr_s.at[a, k], (g, pd))

    def finish(a, zf, zr, out):
        value = zf[dh]
        for k, pd in line:
            remote(zr.at[k], zr.at[k], zs_s.at[a, k], zr_s.at[a, k], (g, pd)).wait_recv()
            value = value + zr[k].astype(f32)
        out[...] = value

    loads[0].wait()
    for n in range(0, w2_v.shape[0], tile):
        wt_v[:, n : n + tile] = w2_v[n : n + tile, :].T
    loads[1].wait()
    loads[2].wait()
    def hand_over():
        loads[4].wait()
        loads[5].wait()
        for k, pd in owners:
            src = (d + D - k) % D
            remote(eb.at[g, src], eb.at[g, src], e1s.at[0, k], e1r.at[0, k], (g, pd)).wait_recv()
            remote(ib.at[g, src], ib.at[g, src], e1s.at[1, k], e1r.at[1, k], (g, pd)).wait_recv()
        for k, pg in groups:
            send(eb.at[g], eb.at[g], e2s.at[0, k], e2r.at[0, k], (pg, d))
            send(ib.at[g], ib.at[g], e2s.at[1, k], e2r.at[1, k], (pg, d))

    for only in order:
        away(only, 0, h_v, True, og_v, cs2, cr2)
    for only in order:
        home(only, 0, h_v, True, og_v, cr2, xs2, xr2, kp2)
    hand_over()

    def back_tile(t, _):
        rows = pl.ds(pl.multiple_of(t * tile, tile), tile)
        back = jnp.dot(og_v[rows, :], wt_v[...], preferred_element_type=f32)
        keep = h_v[rows, :].astype(f32) > 0
        dh_v[rows, :] = jnp.where(keep, back, jnp.zeros_like(back)).astype(bf16)
        return 0

    lax.fori_loop(0, tokens // tile, back_tile, 0)

    loads[3].wait()
    for only in order:
        away(only, 1, x_v, False, dh_v, cs1, cr1)
    for only in order:
        home(only, 1, x_v, False, dh_v, cr1, xs1, xr1, kp1)
    along(0, xr2, kp2, zs2, zf2, zr2)

    for k, pg in groups:
        src = (g + G - k) % G
        remote(eb.at[src], eb.at[src], e2s.at[0, k], e2r.at[0, k], (pg, d)).wait_recv()
        remote(ib.at[src], ib.at[src], e2s.at[1, k], e2r.at[1, k], (pg, d)).wait_recv()
    cap = eb.shape[2]
    pack = LANES // cap
    owned = tg_v.shape[0]

    def owned_tile(t, _):
        start = pl.multiple_of(t * tile, tile)
        rows = pl.ds(start, tile)
        wanted = start + lax.broadcasted_iota(jnp.int32, (tile, LANES), 0)
        total = jnp.zeros((tile, eb.shape[3]), f32)
        for q in range(G):
            parts = []
            for s in range(0, D, pack):
                ids = ib[q, s]
                for e in range(1, pack):
                    ids = jnp.maximum(ids, ib[q, s + e])
                hit = wanted == ids[0:1, :]
                parts.append(jnp.where(hit, 1.0, 0.0).astype(bf16))
            onehot = jnp.concatenate(parts, axis=1)
            total = total + jnp.dot(
                onehot, eb[q].reshape(D * cap, eb.shape[3]), preferred_element_type=f32
            )
        tg_v[rows, :] = total
        return 0

    lax.fori_loop(0, owned // tile, owned_tile, 0)
    stores = [local(tg_v, tg_hbm, 0)]
    for store in stores:
        store.start()

    along(1, xr1, kp1, zs1, zf1, zr1)
    finish(0, zf2, zr2, g2_ref)
    finish(1, zf1, zr1, g1_ref)
    for copy in pending:
        copy.wait_send()
    for store in stores:
        store.wait()


def update(g1_in, g2_in, sum_in, tab_in, st_in, g1_out, g2_out, tab_out, st_out):
    g1_out[...] = g1_in[...]
    g2_out[...] = g2_in[...]
    total = sum_in[...]
    state = st_in[...] + total * total
    st_out[...] = state
    tab_out[...] = tab_in[...] - learn_rate * total / (jnp.sqrt(state) + epsilon)


def solution(mesh):
    G, D = mesh.shape["grp"], mesh.shape["dev"]

    def on_device(
        layer_input, hidden_pre, out_grad, second_weight,
        row_grads, row_ids, block_counts, emb_table, adagrad_state,
    ):
        T, IN = layer_input.shape
        HID, OUT = second_weight.shape
        E = row_grads.shape[1]
        cap = row_grads.shape[0] // D
        owned = emb_table.shape[0]
        GX, DH = G // 2, D // 2
        pack = LANES // cap
        R1, R2 = IN // (G * D), HID // (G * D)
        lane = jnp.arange(LANES, dtype=jnp.int32)
        mine = lax.axis_index("dev") % pack
        usable = (lane[None, :] % cap < block_counts[:, None]) & (lane[None, :] // cap == mine)
        ids = jnp.where(usable, jnp.tile(row_ids.reshape(D, cap), (1, pack)), -1)
        ids = ids[:, None, :]
        f32, bf16 = jnp.float32, jnp.bfloat16

        def stages(R, N):
            return [
                pltpu.VMEM((GX, D * R, N), f32),
                pltpu.VMEM((GX, D * R, N), f32),
                pltpu.VMEM((GX, 2, DH, R, N), bf16),
                pltpu.VMEM((GX * 2, DH, R, N), bf16),
                pltpu.VMEM((2, DH, R, N), f32),
                pltpu.VMEM((DH, R, N), bf16),
                pltpu.VMEM((DH, R, N), f32),
                pltpu.VMEM((DH, R, N), bf16),
            ]

        hbm = pl.BlockSpec(memory_space=pltpu.HBM)
        vmem = pl.BlockSpec(memory_space=pltpu.VMEM)
        dma = pltpu.SemaphoreType.DMA
        g1, g2, summed = pl.pallas_call(
            functools.partial(kernel, G, D),
            out_shape=[
                jax.ShapeDtypeStruct((R1, HID), f32),
                jax.ShapeDtypeStruct((R2, OUT), f32),
                jax.ShapeDtypeStruct(emb_table.shape, f32),
            ],
            in_specs=[hbm] * 6,
            out_specs=[vmem, vmem, hbm],
            scratch_shapes=[
                pltpu.VMEM((T, IN), bf16),
                pltpu.VMEM((T, HID), bf16),
                pltpu.VMEM((T, OUT), bf16),
                pltpu.VMEM((HID, OUT), bf16),
                pltpu.VMEM((OUT, HID), bf16),
                pltpu.VMEM((owned, E), f32),
                pltpu.VMEM((T, HID), bf16),
                pltpu.VMEM((D * R1, T), bf16),
                pltpu.VMEM((G, D, cap, E), bf16),
                pltpu.VMEM((G, D, 1, LANES), jnp.int32),
                *stages(R2, OUT),
                *stages(R1, HID),
                dma((8,)),
                dma((2, GX)), dma((2, GX)),
                dma((2, GX * 2)), dma((2, GX * 2)),
                dma((2, DH)), dma((2, DH)),
                dma((2, D)), dma((2, D)),
                dma((2, G)), dma((2, G)),
            ],
            compiler_params=pltpu.CompilerParams(
                collective_id=0, has_side_effects=True, vmem_limit_bytes=60 * 1024 * 1024
            ),
        )(
            layer_input, hidden_pre, out_grad, second_weight,
            row_grads.reshape(D, cap, E), ids,
        )
        steps = 4
        rows = pl.BlockSpec((owned // steps, E), lambda i: (i, 0))
        part1 = pl.BlockSpec((R1, HID // steps), lambda i: (0, i))
        part2 = pl.BlockSpec((R2, OUT // steps), lambda i: (0, i))
        return pl.pallas_call(
            update,
            grid=(steps,),
            out_shape=[
                jax.ShapeDtypeStruct((R1, HID), f32),
                jax.ShapeDtypeStruct((R2, OUT), f32),
                jax.ShapeDtypeStruct(emb_table.shape, f32),
                jax.ShapeDtypeStruct(adagrad_state.shape, f32),
            ],
            in_specs=[part1, part2, rows, rows, rows],
            out_specs=[part1, part2, rows, rows],
        )(g1, g2, summed, emb_table, adagrad_state)

    return jax.shard_map(
        on_device,
        mesh=mesh,
        in_specs=(
            P(("grp", "dev"), None),
            P(("grp", "dev"), None),
            P(("grp", "dev"), None),
            P(),
            P(("grp", "dev"), None),
            P(("grp", "dev")),
            P(("grp", "dev")),
            P("dev", None),
            P("dev", None),
        ),
        out_specs=(P(("grp", "dev"), None), P(("grp", "dev"), None), P("dev", None), P("dev", None)),
        check_vma=False,
    )
```

profile of v0, /device:TPU:0, one launch (start us, length us, event | category | flops | bytes accessed | tf_op | source)
XLA Modules:
  0.0 52.5 jit_solution(6414715930289742742)
XLA Ops:
  0.7 0.8 %tile.10 = s32[8,64]{1,0:T(8,128)S(1)} reshape(s32[512]{0:T(512)} %param.14) | data formatting | bytes 4096 | tf_op jit(solution)/shard_map/tile | solution.py:268
  1.4 0.1 tile.12
  1.5 1.3 %and_select_fusion.ids_hbm = s32[8,1,128]{2,1,0:T(1,128)} fusion(s32[8,1,128]{2,1,0:T(1,128)S(1)} %tile.12, pred[128]{0:T(512)(128)(4,1)S(1)} %fusion, s32[128]{0:T(128)S(1)} %and_select_fusion.2, s32[8]{0:T(128)} %param.15), kind=kLoop, calls=%fused_computation | loop fusion | flops 3072 | bytes 8864 | tf_op jit(solution)/shard_map/jit(_where)/select_n | solution.py:268
  2.8 45.6 %shard_map.120 = (f32[32,1024]{1,0:T(8,128)}, f32[32,512]{1,0:T(8,128)}, f32[2048,128]{1,0:T(8,128)}) custom-call(bf16[2048,1024]{1,0:T(8,128)(2,1)} %x_hbm.1, bf16[2048,1024]{1,0:T(8,128)(2,1)} %h_hbm.1, bf16[2048,512]{1,0:T(8,128)(2,1)} %og_hbm.1, bf16[1024,512]{1,0:T(8,128)(2,1)} %w2_hbm.1, bf16[8,64,128]{2,1,0:T(8,128)(2,1)} %bitcast.1, ...), custom_call_target="tpu_custom_call" | custom-call | tf_op jit(solution)/shard_map/pallas_call | solution.py:287
  48.5 4.1 %shard_map.121 = (f32[32,1024]{1,0:T(8,128)}, f32[32,512]{1,0:T(8,128)}, f32[2048,128]{1,0:T(8,128)}, f32[2048,128]{1,0:T(8,128)}) custom-call(f32[32,1024]{1,0:T(8,128)} %get-tuple-element.7.g1_in, f32[32,512]{1,0:T(8,128)} %get-tuple-element.8.g2_in, f32[2048,128]{1,0:T(8,128)} %get-tuple-element.9.sum_in, f32[2048,128]{1,0:T(8,128)} %tab_in.1, ...), custom_call_target="tpu_custom_call" | custom-call | tf_op jit(solution)/shard_map/pallas_call | solution.py:327
  (3 shorter events, 0.0 us)
where the time goes:
time: 52.8 us; the launch traced here: 52.5 us
  Pallas kernels  49.7 us (94%)
  other arithmetic  1.33 us (3%)
  local copies, waits for them, and re-layouts  0.85 us (2%)
  between operations  0.66 us (1%)
    pallas_call x1, Pallas kernels, on_device(): pl.pallas_call(functools.partial(kernel, G, D), out_shape=[jax.ShapeDtype...  45.6 us
    pallas_call x1, Pallas kernels, on_device(): pl.pallas_call(update, grid=(steps,), out_shape=[jax.ShapeDtypeStruct((R1...  4.09 us
    select_n x1, other arithmetic, on_device(): ids = jnp.where(usable, jnp.tile(row_ids.reshape(D, cap), (1, pack)), -1)  1.32 us

commit v1 on v0

v1 whole, which is shorter than its diff:
```python
import functools

import jax
import jax.numpy as jnp
from jax import lax
from jax.experimental import pallas as pl
from jax.experimental.pallas import tpu as pltpu
from jax.sharding import PartitionSpec as P

learn_rate = 0.5
epsilon = 1e-08
MESH = pl.DeviceIdType.MESH
LANES = 128
f32, bf16 = jnp.float32, jnp.bfloat16


def kernel(
    G, D, PW,
    x_hbm, h_hbm, og_hbm, w2_hbm, rg_hbm, ids_hbm, cnt_hbm, tab_hbm, st_hbm,
    g1_ref, g2_ref, tab_ref, st_ref,
    x_v, h_v, og_v, w2_v, dh_v, tab_v, st_v, ids_v, cnt_s,
    hv, cs, cr, xs, xr, ys, yr, fv, zs, zr,
    sb, eb, eo, ij, ir, ib, iz, io,
    lsem, cs_s, cr_s, xs_s, xr_s, ys_s, yr_s, zs_s, zr_s,
    es_s, er_s, ez_s, ez_r,
):
    GX, DH = G // 2, D // 2
    assert GX == 2
    g, d = lax.axis_index("grp"), lax.axis_index("dev")
    gx, c = g // 2, g % 2
    dh, dl = d // 2, d % 2
    tokens = x_v.shape[0]
    n1, n2 = dh_v.shape[1], og_v.shape[1]
    R = g1_ref.shape[0]
    DR = D * R
    first_core = c == 0

    def pick(a, b):
        return jnp.where(first_core, a, b)

    def local(src, dst, i):
        return pltpu.make_async_copy(src, dst, lsem.at[i])

    half = tokens // 2
    other_c = (c + 1) % 2

    def group_cols(gxx, cc):
        return pl.ds(pl.multiple_of((gxx * 2 + cc) * DR, DR), DR)

    loads = {}

    def load(name, src, dst):
        copy = local(src, dst, len(loads))
        loads[name] = copy
        copy.start()

    load("ids", ids_hbm, ids_v)
    load("cnt", cnt_hbm, cnt_s)
    load("og", og_hbm, og_v)
    for k in range(GX):
        load(("h", "a", k), h_hbm.at[:, group_cols(k, other_c)], h_v.at[:, group_cols(k, other_c)])
    for k in range(GX):
        load(("h", "h", k), h_hbm.at[:, group_cols(k, c)], h_v.at[:, group_cols(k, c)])
    load("w2", w2_hbm, w2_v)
    load("x", x_hbm, x_v)
    load("own", rg_hbm.at[:, dl], sb.at[:, 0, dl])
    load("tab", tab_hbm, tab_v)
    load("st", st_hbm, st_v)

    odl = (dl + 1) % 2
    core_peer = (gx * 2 + other_c, d)
    x_peer = (((gx + 1) % GX) * 2 + c, d)
    y_peer = (g, dh * 2 + odl)
    line = [(k, ((dh + k) % DH) * 2 + dl) for k in range(1, DH)]
    first_peer = (pick(x_peer[0], y_peer[0]), pick(x_peer[1], y_peer[1]))
    second_peer = (pick(y_peer[0], x_peer[0]), pick(y_peer[1], x_peer[1]))
    peers = [core_peer, x_peer, y_peer] + [(g, pd) for k, pd in line]
    barrier = pltpu.get_barrier_semaphore()
    for peer in peers:
        pl.semaphore_signal(barrier, inc=1, device_id=peer, device_id_type=MESH)

    loads["ids"].wait()
    loads["cnt"].wait()
    lane = lax.broadcasted_iota(jnp.int32, (1, LANES), 1)
    side = lane // (LANES // 2)
    for z in range(DH):
        count = jnp.where(side == 0, cnt_s[2 * z], cnt_s[2 * z + 1])
        row = jnp.where(lane % (LANES // 2) < count, ids_v[z : z + 1, :], -1)
        ib[z, 0] = jnp.where(side == dl, row, -1)
        ij[z] = pltpu.roll(jnp.where(side == odl, row, -1), LANES // 2, 1)

    pl.semaphore_wait(barrier, len(peers))

    def remote(src, dst, ss, rs, to):
        return pltpu.make_async_remote_copy(
            src_ref=src, dst_ref=dst, send_sem=ss, recv_sem=rs, device_id=to, device_id_type=MESH
        )

    pending = []

    def send(*args):
        copy = remote(*args)
        copy.start()
        pending.append(copy)

    def landed(dst, ss, rs):
        remote(dst, dst, ss, rs, core_peer).wait_recv()

    send(rg_hbm.at[:, odl], sb.at[:, 0, dl], es_s.at[0], er_s.at[0], y_peer)
    send(ij, ir, es_s.at[1], er_s.at[1], y_peer)
    send(rg_hbm.at[:, dl], sb.at[:, 1, dl], es_s.at[2], er_s.at[2], x_peer)

    def slots_x():
        landed(sb.at[:, 0, odl], es_s.at[0], er_s.at[0])
        landed(ir, es_s.at[1], er_s.at[1])
        for z in range(DH):
            ib[z, 0] = jnp.maximum(ib[z, 0], ir[z])
        send(ib.at[:, 0], ib.at[:, 1], es_s.at[3], er_s.at[3], x_peer)
        send(sb.at[:, 0, odl], sb.at[:, 1, odl], es_s.at[4], er_s.at[4], x_peer)

    def slots_z():
        loads["own"].wait()
        landed(ib.at[:, 1], es_s.at[3], er_s.at[3])
        landed(sb.at[:, 1, dl], es_s.at[2], er_s.at[2])
        landed(sb.at[:, 1, odl], es_s.at[4], er_s.at[4])
        for k, pd in line[::-1]:
            t = (dh + k) % DH
            send(ib.at[t], iz.at[k], ez_s.at[0, k], ez_r.at[0, k], (g, pd))
            send(sb.at[t], eb.at[k], ez_s.at[1, k], ez_r.at[1, k], (g, pd))
        send(ib.at[dh], io.at[0], es_s.at[5], er_s.at[5], core_peer)
        send(sb.at[dh], eo.at[0], es_s.at[6], er_s.at[6], core_peer)

    def slots_core():
        for k, pd in line:
            landed(iz.at[k], ez_s.at[0, k], ez_r.at[0, k])
            landed(eb.at[k], ez_s.at[1, k], ez_r.at[1, k])
        rest = pl.ds(1, DH - 1)
        send(iz.at[rest], io.at[rest], es_s.at[7], er_s.at[7], core_peer)
        send(eb.at[rest], eo.at[rest], es_s.at[8], er_s.at[8], core_peer)

    def slots_all():
        landed(io.at[0], es_s.at[5], er_s.at[5])
        landed(eo.at[0], es_s.at[6], er_s.at[6])
        rest = pl.ds(1, DH - 1)
        landed(io.at[rest], es_s.at[7], er_s.at[7])
        landed(eo.at[rest], es_s.at[8], er_s.at[8])

    contract = (((0,), (0,)), ((), ()))

    def left(src, cc, relu):
        block = jnp.concatenate([src[:, group_cols(k, cc)] for k in range(GX)], axis=1)
        if relu:
            block = jnp.maximum(block, jnp.zeros_like(block))
        return block

    def away(n, width, src, relu, rhs, at):
        value = lax.dot_general(
            left(src, other_c, relu), rhs[:, at : at + width], contract, preferred_element_type=f32
        )
        for s in range(width // PW):
            for k in range(GX):
                cs[n + s, k] = value[k * DR : (k + 1) * DR, s * PW : (s + 1) * PW]
            send(cs.at[n + s], cr.at[n + s], cs_s.at[n + s], cr_s.at[n + s], core_peer)

    def home(n, width, src, relu, rhs, at):
        value = lax.dot_general(
            left(src, c, relu), rhs[:, at : at + width], contract, preferred_element_type=f32
        )
        for s in range(width // PW):
            for k in range(GX):
                hv[n + s, k] = value[k * DR : (k + 1) * DR, s * PW : (s + 1) * PW]

    p_me, q_me = pick(gx, dl), pick(dl, gx)
    p_no, q_no = 1 - p_me, 1 - q_me

    def chip_sum(n, p, q, b):
        k = pick(p, q)
        rows = pl.ds(pl.multiple_of((b * 2 + pick(q, p)) * R, R), R)
        return hv[n, k, rows, :] + cr[n, k, rows, :]

    def step_chip(n):
        landed(cr.at[n], cs_s.at[n], cr_s.at[n])
        for q in range(2):
            for b in range(DH):
                xs[n, q, b] = chip_sum(n, p_no, q, b).astype(bf16)
        send(xs.at[n], xr.at[n], xs_s.at[n], xr_s.at[n], first_peer)

    def step_first(n):
        landed(xr.at[n], xs_s.at[n], xr_s.at[n])
        for b in range(DH):
            ys[n, b] = (chip_sum(n, p_me, q_no, b) + xr[n, q_no, b].astype(f32)).astype(bf16)
        send(ys.at[n], yr.at[n], ys_s.at[n], yr_s.at[n], second_peer)
        for b in range(DH):
            fv[n, b] = chip_sum(n, p_me, q_me, b) + xr[n, q_me, b].astype(f32)

    def step_second(n):
        landed(yr.at[n], ys_s.at[n], yr_s.at[n])
        for b in range(DH):
            value = fv[n, b] + yr[n, b].astype(f32)
            zs[n, b] = value.astype(bf16)
            fv[n, b] = value
        for k, pd in line[::-1]:
            send(zs.at[n, (dh + k) % DH], zr.at[n, k], zs_s.at[n, k], zr_s.at[n, k], (g, pd))

    def step_line(n, out, at):
        value = fv[n, dh]
        for k, pd in line:
            landed(zr.at[n, k], zs_s.at[n, k], zr_s.at[n, k])
            value = value + zr[n, k].astype(f32)
        out[:, at : at + PW] = value

    def back(rows, cols):
        value = lax.dot_general(
            og_v[rows, :], w2_v[cols, :], (((1,), (1,)), ((), ())), preferred_element_type=f32
        )
        keep = h_v[rows, cols].astype(f32) > 0
        dh_v[rows, cols] = jnp.where(keep, value, jnp.zeros_like(value)).astype(bf16)

    owned = tab_v.shape[0]
    tile = 256

    def table_tiles(first, last):
        def body(t, _):
            start = pl.multiple_of(t * tile, tile)
            rows = pl.ds(start, tile)
            wanted = start + lax.broadcasted_iota(jnp.int32, (tile, LANES), 0)
            total = jnp.zeros((tile, tab_v.shape[1]), f32)
            for k in range(DH):
                parts = []
                blocks = []
                for who in range(2):
                    for a in range(GX):
                        if who:
                            ids, block = io[k, a], eo[k, a]
                        elif k:
                            ids, block = iz[k, a], eb[k, a]
                        else:
                            ids, block = ib[dh, a], sb[dh, a]
                        hit = wanted == ids
                        parts.append(jnp.where(hit, 1.0, 0.0).astype(bf16))
                        blocks.append(block.reshape(LANES, tab_v.shape[1]))
                total = total + jnp.dot(
                    jnp.concatenate(parts, axis=1),
                    jnp.concatenate(blocks, axis=0),
                    preferred_element_type=f32,
                )
            state = st_v[rows, :] + total * total
            st_ref[rows, :] = state
            tab_ref[rows, :] = tab_v[rows, :] - learn_rate * total / (jnp.sqrt(state) + epsilon)
            return 0

        lax.fori_loop(first, last, body, 0)

    W = 2 * PW
    loads["og"].wait()
    for k in range(GX):
        loads[("h", "a", k)].wait()
    away(0, W, h_v, True, og_v, 0)
    for k in range(GX):
        loads[("h", "h", k)].wait()
    home(0, W, h_v, True, og_v, 0)
    loads["w2"].wait()
    back(pl.ds(0, half), pl.ds(0, W))
    slots_x()
    step_chip(0)
    step_chip(1)
    back(pl.ds(half, half), pl.ds(0, W))
    loads["x"].wait()
    away(2, W, x_v, False, dh_v, 0)
    home(2, W, x_v, False, dh_v, 0)
    slots_z()
    back(pl.ds(0, half), pl.ds(W, W))
    step_chip(2)
    step_chip(3)
    step_first(0)
    back(pl.ds(half, half), pl.ds(W, W))
    step_first(1)
    away(4, W, x_v, False, dh_v, W)
    home(4, W, x_v, False, dh_v, W)
    step_chip(4)
    step_chip(5)
    step_second(0)
    step_first(2)
    slots_core()
    step_second(1)
    step_first(3)
    step_second(2)
    loads["tab"].wait()
    loads["st"].wait()
    slots_all()
    tiles = owned // tile
    table_tiles(0, tiles // 2)
    step_first(4)
    step_second(3)
    table_tiles(tiles // 2, tiles)
    step_first(5)
    step_second(4)
    step_line(0, g2_ref, 0)
    step_line(1, g2_ref, PW)
    step_second(5)
    step_line(2, g1_ref, 0)
    step_line(3, g1_ref, PW)
    step_line(4, g1_ref, W)
    step_line(5, g1_ref, W + PW)
    for copy in pending:
        copy.wait_send()


def solution(mesh):
    G, D = mesh.shape["grp"], mesh.shape["dev"]

    def on_device(
        layer_input, hidden_pre, out_grad, second_weight,
        row_grads, row_ids, block_counts, emb_table, adagrad_state,
    ):
        T, IN = layer_input.shape
        HID, OUT = second_weight.shape
        E = row_grads.shape[1]
        cap = row_grads.shape[0] // D
        assert LANES // cap == 2
        GX, DH = G // 2, D // 2
        R1, R2 = IN // (G * D), HID // (G * D)
        PW = OUT // 2
        N = (OUT + HID) // PW
        hbm = pl.BlockSpec(memory_space=pltpu.HBM)
        vmem = pl.BlockSpec(memory_space=pltpu.VMEM)
        dma = pltpu.SemaphoreType.DMA
        return pl.pallas_call(
            functools.partial(kernel, G, D, PW),
            out_shape=[
                jax.ShapeDtypeStruct((R1, HID), f32),
                jax.ShapeDtypeStruct((R2, OUT), f32),
                jax.ShapeDtypeStruct(emb_table.shape, f32),
                jax.ShapeDtypeStruct(adagrad_state.shape, f32),
            ],
            in_specs=[hbm] * 9,
            out_specs=[vmem] * 4,
            scratch_shapes=[
                pltpu.VMEM((T, IN), bf16),
                pltpu.VMEM((T, HID), bf16),
                pltpu.VMEM((T, OUT), bf16),
                pltpu.VMEM((HID, OUT), bf16),
                pltpu.VMEM((T, HID), bf16),
                pltpu.VMEM(emb_table.shape, f32),
                pltpu.VMEM(adagrad_state.shape, f32),
                pltpu.VMEM((DH, LANES), jnp.int32),
                pltpu.SMEM((D,), jnp.int32),
                pltpu.VMEM((N, GX, D * R1, PW), f32),
                pltpu.VMEM((N, GX, D * R1, PW), f32),
                pltpu.VMEM((N, GX, D * R1, PW), f32),
                pltpu.VMEM((N, 2, DH, R1, PW), bf16),
                pltpu.VMEM((N, 2, DH, R1, PW), bf16),
                pltpu.VMEM((N, DH, R1, PW), bf16),
                pltpu.VMEM((N, DH, R1, PW), bf16),
                pltpu.VMEM((N, DH, R1, PW), f32),
                pltpu.VMEM((N, DH, R1, PW), bf16),
                pltpu.VMEM((N, DH, R1, PW), bf16),
                pltpu.VMEM((DH, GX, 2, cap, E), bf16),
                pltpu.VMEM((DH, GX, 2, cap, E), bf16),
                pltpu.VMEM((DH, GX, 2, cap, E), bf16),
                pltpu.VMEM((DH, 1, LANES), jnp.int32),
                pltpu.VMEM((DH, 1, LANES), jnp.int32),
                pltpu.VMEM((DH, GX, 1, LANES), jnp.int32),
                pltpu.VMEM((DH, GX, 1, LANES), jnp.int32),
                pltpu.VMEM((DH, GX, 1, LANES), jnp.int32),
                dma((16,)),
                dma((N,)), dma((N,)),
                dma((N,)), dma((N,)),
                dma((N,)), dma((N,)),
                dma((N, DH)), dma((N, DH)),
                dma((9,)), dma((9,)),
                dma((2, DH)), dma((2, DH)),
            ],
            compiler_params=pltpu.CompilerParams(
                collective_id=0, has_side_effects=True, vmem_limit_bytes=52 * 1024 * 1024
            ),
        )(
            layer_input, hidden_pre, out_grad, second_weight,
            row_grads.reshape(DH, 2, cap, E), row_ids.reshape(DH, LANES), block_counts,
            emb_table, adagrad_state,
        )

    return jax.shard_map(
        on_device,
        mesh=mesh,
        in_specs=(
            P(("grp", "dev"), None),
            P(("grp", "dev"), None),
            P(("grp", "dev"), None),
            P(),
            P(("grp", "dev"), None),
            P(("grp", "dev")),
            P(("grp", "dev")),
            P("dev", None),
            P("dev", None),
        ),
        out_specs=(P(("grp", "dev"), None), P(("grp", "dev"), None), P("dev", None), P("dev", None)),
        check_vma=False,
    )
```

time: 52.8 us -> 44.1 us (0.84)
  Pallas kernels: 49.7 us -> 36.4 us
  local copies, waits for them, and re-layouts: 0.85 us -> 6.75 us
  other arithmetic: 1.33 us -> 0 us
    pallas_call x2 -> x1, Pallas kernels: 49.7 us -> 36.4 us  [on_device(): pl.pallas_call(functools.partial(kernel, G, D, PW), out_shape=[jax.ShapeD...]
    unnamed x0 -> x10, local copies, waits for them, and re-layouts: none -> 6.75 us
    select_n x2 -> x0, other arithmetic: 1.33 us -> none  [the longest x1 1.32 us: on_device(): ids = jnp.where(usable, jnp.tile(row_ids.reshape(D, cap), (1, pack)), -1)]
    another operation x3 -> x0, local copies, waits for them, and re-layouts: 0.85 us -> none  [on_device(): ids = jnp.where(usable, jnp.tile(row_ids.reshape(D, cap), (1, pack)), -1)]
where the time goes in v1:
time: 44.1 us; the launch traced here: 43.8 us
  Pallas kernels  36.4 us (83%)
  local copies, waits for them, and re-layouts  6.75 us (15%)
  between operations  0.65 us (1%)
    pallas_call x1, Pallas kernels, on_device(): pl.pallas_call(functools.partial(kernel, G, D, PW), out_shape=[jax.ShapeD...  36.4 us
    unnamed x10, local copies, waits for them, and re-layouts  6.75 us

profile of v1, /device:TPU:0, one launch (start us, length us, event | category | flops | bytes accessed | tf_op | source)
XLA Modules:
  0.0 43.8 jit_solution(6036191041799965522)
XLA Ops:
  0.6 0.0 copy-start
  0.6 0.9 %copy-done = bf16[512,128]{1,0:T(8,128)(2,1)S(1)} copy-done((bf16[512,128]{1,0:T(8,128)(2,1)S(1)}, bf16[512,128]{1,0:T(8,128)(2,1)}, u32[]{:S(2)}) %copy-start) | copy-done | bytes 131096
  1.5 0.0 copy-start.1
  1.5 0.7 %copy-done.1 = s32[512]{0:T(512)S(1)} copy-done((s32[512]{0:T(512)S(1)}, s32[512]{0:T(512)}, u32[]{:S(2)}) %copy-start.1) | copy-done | bytes 2072
  2.2 0.0 copy-start.2
  2.2 0.7 %copy-done.2 = s32[8]{0:T(128)S(1)} copy-done((s32[8]{0:T(128)S(1)}, s32[8]{0:T(128)}, u32[]{:S(2)}) %copy-start.2) | copy-done | bytes 56
  2.9 36.4 %shard_map.120 = (f32[32,1024]{1,0:T(8,128)S(1)}, f32[32,512]{1,0:T(8,128)S(1)}, f32[2048,128]{1,0:T(8,128)S(1)}, f32[2048,128]{1,0:T(8,128)}) custom-call(bf16[2048,1024]{1,0:T(8,128)(2,1)} %x_hbm.1, bf16[2048,1024]{1,0:T(8,128)(2,1)} %h_hbm.1, bf16[2048,512]{1,0:T(8,128)(2,1)} %og_hbm.1, bf16[1024,512]{1,0:T(8,128)(2,1)} %w2_hbm.1, ...), custom_call_target="tpu_custom_call" | custom-call | tf_op jit(solution)/shard_map/pallas_call | solution.py:328
  39.3 0.7 %copy.17 = f32[32,1024]{1,0:T(8,128)} copy(f32[32,1024]{1,0:T(8,128)S(1)} %get-tuple-element.8) | data formatting | bytes 262144
  40.0 0.6 %copy.18 = f32[32,512]{1,0:T(8,128)} copy(f32[32,512]{1,0:T(8,128)S(1)} %get-tuple-element.9) | data formatting | bytes 131072
  40.6 1.0 %copy.19 = f32[2048,128]{1,0:T(8,128)} copy(f32[2048,128]{1,0:T(8,128)S(1)} %get-tuple-element.10) | data formatting | bytes 2097152
  41.6 2.3 %copy.20 = f32[2048,128]{1,0:T(8,128)} copy(f32[2048,128]{1,0:T(8,128)} %get-tuple-element.11) | data formatting | bytes 2097152
Async XLA Ops:
  0.6 0.9 %copy-start = (bf16[512,128]{1,0:T(8,128)(2,1)S(1)}, bf16[512,128]{1,0:T(8,128)(2,1)}, u32[]{:S(2)}) copy-start(bf16[512,128]{1,0:T(8,128)(2,1)} %param.13) | copy-start | bytes 393220
  1.5 0.7 %copy-start.1 = (s32[512]{0:T(512)S(1)}, s32[512]{0:T(512)}, u32[]{:S(2)}) copy-start(s32[512]{0:T(512)} %param.14) | copy-start | bytes 6148
  2.2 0.7 %copy-start.2 = (s32[8]{0:T(128)S(1)}, s32[8]{0:T(128)}, u32[]{:S(2)}) copy-start(s32[8]{0:T(128)} %cnt_hbm.1) | copy-start | bytes 100

commit v2 on v1

v2 whole, which is shorter than its diff:
```python
import functools

import jax
import jax.numpy as jnp
from jax import lax
from jax.experimental import pallas as pl
from jax.experimental.pallas import tpu as pltpu
from jax.sharding import PartitionSpec as P

learn_rate = 0.5
epsilon = 1e-08
MESH = pl.DeviceIdType.MESH
LANES = 128
f32, bf16 = jnp.float32, jnp.bfloat16


def kernel(
    G, D,
    x_hbm, h_hbm, og_hbm, w2_hbm, rg_hbm, ids_hbm, cnt_hbm, tab_hbm, st_hbm,
    g1_ref, g2_ref, tab_ref, st_ref,
    x_v, h_v, og_v, w2_v, dh_v, ids_v, cnt_s,
    hv, cs, cr, xs, xr, ys, yr, fv, zs, zr,
    sb, eb, eo, ij, iw, iz, io,
    sums, lsem, s_sem, c_sem, x_sem, y_sem, z_sem, e_sem,
):
    GX, DH = G // 2, D // 2
    assert GX == 2
    g, d = lax.axis_index("grp"), lax.axis_index("dev")
    gx, c = g // 2, g % 2
    dh, dl = d // 2, d % 2
    tokens = x_v.shape[0]
    half = tokens // 2
    R = g1_ref.shape[0]
    DR = D * R
    U = LANES
    first_core = c == 0

    def pick(a, b):
        return jnp.where(first_core, a, b)

    other_c = (c + 1) % 2

    def group_cols(k, cc):
        return pl.ds(pl.multiple_of((k * 2 + cc) * DR, DR), DR)

    loads = {}

    def load(name, src, dst):
        copy = pltpu.make_async_copy(src, dst, lsem.at[len(loads)])
        loads[name] = copy
        copy.start()

    load("ids", ids_hbm, ids_v)
    load("cnt", cnt_hbm, cnt_s)
    for t in range(2):
        rows = pl.ds(t * half, half)
        load(("og", t), og_hbm.at[rows], og_v.at[rows])
        for k in range(GX):
            cols = group_cols(k, other_c)
            load(("h", "away", t, k), h_hbm.at[rows, cols], h_v.at[rows, cols])
    for k in range(GX):
        cols = group_cols(k, c)
        load(("h", "home", k), h_hbm.at[:, cols], h_v.at[:, cols])
    load("w2", w2_hbm, w2_v)
    load("x", x_hbm, x_v)
    load("own", rg_hbm.at[:, dl], sb.at[:, gx, dl])
    load("tab", tab_hbm, tab_ref)
    load("st", st_hbm, st_ref)

    odl = (dl + 1) % 2
    core_peer = (gx * 2 + other_c, d)
    x_peer = (((gx + 1) % GX) * 2 + c, d)
    y_peer = (g, dh * 2 + odl)
    diagonal = (x_peer[0], y_peer[1])
    line = [(k, ((dh + k) % DH) * 2 + dl) for k in range(1, DH)]
    first_peer = (pick(x_peer[0], y_peer[0]), pick(x_peer[1], y_peer[1]))
    second_peer = (pick(y_peer[0], x_peer[0]), pick(y_peer[1], x_peer[1]))
    peers = [core_peer, x_peer, y_peer, diagonal] + [(g, pd) for k, pd in line]
    barrier = pltpu.get_barrier_semaphore()
    for peer in peers:
        pl.semaphore_signal(barrier, inc=1, device_id=peer, device_id_type=MESH)

    loads["ids"].wait()
    loads["cnt"].wait()
    lane = lax.broadcasted_iota(jnp.int32, (1, LANES), 1)
    side = lane // (LANES // 2)
    for z in range(DH):
        count = jnp.where(side == 0, cnt_s[2 * z], cnt_s[2 * z + 1])
        row = jnp.where(lane % (LANES // 2) < count, ids_v[z : z + 1, :], -1)
        ij[0, z] = jnp.where(side == dl, row, -1)
        ij[1, z] = pltpu.roll(jnp.where(side == odl, row, -1), LANES // 2, 1)
        iw[z, gx, dl] = ij[0, z]

    pl.semaphore_wait(barrier, len(peers))

    def remote(src, dst, ss, rs, to):
        return pltpu.make_async_remote_copy(
            src_ref=src, dst_ref=dst, send_sem=ss, recv_sem=rs, device_id=to, device_id_type=MESH
        )

    def send(src, dst, i, rs, to):
        remote(src, dst, s_sem.at[i], rs, to).start()

    def landed(dst, rs):
        remote(dst, dst, s_sem.at[8], rs, core_peer).wait_recv()

    def left_here(src, i):
        remote(src, src, s_sem.at[i], c_sem.at[0], core_peer).wait_send()

    ox = (gx + 1) % GX
    plane = [(y_peer, odl, gx, odl, 1), (x_peer, dl, ox, dl, 0), (diagonal, odl, ox, odl, 1)]
    for i, (to, y, _, _, moved) in enumerate(plane):
        send(ij.at[moved], iw.at[:, gx, dl], 2 * i, e_sem.at[2 * i], to)
        send(rg_hbm.at[:, y], sb.at[:, gx, dl], 2 * i + 1, e_sem.at[2 * i + 1], to)

    def slots_line():
        loads["own"].wait()
        for i, (_, _, a, b, _) in enumerate(plane):
            landed(iw.at[:, a, b], e_sem.at[2 * i])
            landed(sb.at[:, a, b], e_sem.at[2 * i + 1])
        for k, pd in line[::-1]:
            t = (dh + k) % DH
            send(iw.at[t], iz.at[k], 12, e_sem.at[6], (g, pd))
            send(sb.at[t], eb.at[k], 13, e_sem.at[7], (g, pd))
        send(iw.at[dh], io.at[0], 14, e_sem.at[8], core_peer)
        send(sb.at[dh], eo.at[0], 15, e_sem.at[9], core_peer)

    rest = pl.ds(1, DH - 1)

    def slots_core():
        landed(iz.at[rest], e_sem.at[6])
        landed(eb.at[rest], e_sem.at[7])
        send(iz.at[rest], io.at[rest], 16, e_sem.at[10], core_peer)
        send(eb.at[rest], eo.at[rest], 17, e_sem.at[11], core_peer)

    def slots_here(a):
        landed(io.at[rest if a else 0], e_sem.at[8 + 2 * a])
        landed(eo.at[rest if a else 0], e_sem.at[9 + 2 * a])

    contract = (((0,), (0,)), ((), ()))

    def left(src, cc, relu, rows):
        block = jnp.concatenate([src[rows, group_cols(k, cc)] for k in range(GX)], axis=1)
        if relu:
            block = jnp.maximum(block, jnp.zeros_like(block))
        return block

    def product(dst, cc, n, units, src, relu, rhs, at, rows=pl.ds(0, tokens), add=False):
        cols = pl.ds(at * U if isinstance(at, int) else pl.multiple_of(at * U, U), units * U)
        value = lax.dot_general(
            left(src, cc, relu, rows), rhs[rows, cols], contract, preferred_element_type=f32
        )
        for s in range(units):
            for k in range(GX):
                part = value[k * DR : (k + 1) * DR, s * U : (s + 1) * U]
                dst[n + s, k] = dst[n + s, k] + part if add else part

    def send_core(j, n, w):
        p = pl.ds(n, w)
        send(cs.at[p], cr.at[p], 8, c_sem.at[j], core_peer)

    def away_two(j, n, src, rhs, at):
        def body(i, _):
            product(cs, other_c, n + 2 * i, 2, src, False, rhs, at + 2 * i)
            send_core(j + i, n + 2 * i, 2)
            return 0

        lax.fori_loop(0, 2, body, 0)

    p_me, q_me = pick(gx, dl), pick(dl, gx)
    p_no, q_no = 1 - p_me, 1 - q_me

    def chip_sum(n, p, q, b):
        k = pick(p, q)
        rows = pl.ds(pl.multiple_of((b * 2 + pick(q, p)) * R, R), R)
        return hv[n, k, rows, :] + cr[n, k, rows, :]

    pieces = [(0, 2), (2, 2), (4, 2), (6, 2), (8, 2), (10, 1), (11, 1)]

    def chip_landed(j, n, w):
        landed(cr.at[pl.ds(n, w)], c_sem.at[j])

    def step_chip(j):
        n, w = pieces[j]
        at = pl.ds(n, w)
        for u in range(n, n + w):
            for q in range(2):
                for b in range(DH):
                    xs[u, q, b] = chip_sum(u, p_no, q, b).astype(bf16)
        send(xs.at[at], xr.at[at], 9, x_sem.at[j], first_peer)

    def step_first(j):
        n, w = pieces[j]
        at = pl.ds(n, w)
        landed(xr.at[at], x_sem.at[j])
        for u in range(n, n + w):
            for b in range(DH):
                ys[u, b] = (chip_sum(u, p_me, q_no, b) + xr[u, q_no, b].astype(f32)).astype(bf16)
        send(ys.at[at], yr.at[at], 10, y_sem.at[j], second_peer)
        for u in range(n, n + w):
            for b in range(DH):
                fv[u, b] = chip_sum(u, p_me, q_me, b) + xr[u, q_me, b].astype(f32)

    def step_second(j):
        n, w = pieces[j]
        at = pl.ds(n, w)
        landed(yr.at[at], y_sem.at[j])
        for b in range(DH):
            for u in range(n, n + w):
                value = fv[u, b] + yr[u, b].astype(f32)
                zs[b, u] = value.astype(bf16)
                fv[u, b] = value
        for k, pd in line[::-1]:
            send(zs.at[(dh + k) % DH, at], zr.at[k, at], 11, z_sem.at[j], (g, pd))

    def step_line(j):
        n, w = pieces[j]
        landed(zr.at[pl.ds(1, DH - 1), pl.ds(n, w)], z_sem.at[j])
        for u in range(n, n + w):
            value = fv[u, dh]
            for k, pd in line:
                value = value + zr[k, u].astype(f32)
            if u < n2:
                g2_ref[:, u * U : (u + 1) * U] = value
            else:
                g1_ref[:, (u - n2) * U : (u - n2 + 1) * U] = value

    def back(rows, at, units):
        cols = pl.ds(at * U, units * U)
        value = lax.dot_general(
            og_v[rows, :], w2_v[cols, :], (((1,), (1,)), ((), ())), preferred_element_type=f32
        )
        keep = h_v[rows, cols].astype(f32) > 0
        dh_v[rows, cols] = jnp.where(keep, value, jnp.zeros_like(value)).astype(bf16)

    E = tab_ref.shape[1]
    tile = 256
    every = pl.ds(0, tokens)

    def table_tiles(a, first, last):
        def body(t, _):
            start = pl.multiple_of(t * tile, tile)
            rows = pl.ds(start, tile)
            wanted = start + lax.broadcasted_iota(jnp.int32, (tile, LANES), 0)
            total = sums[rows, :] if a else jnp.zeros((tile, E), f32)
            for k in range(1, DH) if a else range(1):
                parts, blocks = [], []
                for ids, block in ((iz[k], eb[k]) if k else (iw[dh], sb[dh]), (io[k], eo[k])):
                    for e in range(GX):
                        hit = wanted == jnp.maximum(ids[e, 0], ids[e, 1])
                        parts.append(jnp.where(hit, 1.0, 0.0).astype(bf16))
                    blocks.append(block.reshape(GX * LANES, E))
                total = total + jnp.dot(
                    jnp.concatenate(parts, axis=1),
                    jnp.concatenate(blocks, axis=0),
                    preferred_element_type=f32,
                )
            if not a:
                sums[rows, :] = total
            else:
                state = st_ref[rows, :] + total * total
                st_ref[rows, :] = state
                tab_ref[rows, :] = tab_ref[rows, :] - learn_rate * total / (jnp.sqrt(state) + epsilon)
            return 0

        lax.fori_loop(first, last, body, 0)

    tiles = tab_ref.shape[0] // tile
    some = tiles // 4
    n2 = og_v.shape[1] // U
    n1 = dh_v.shape[1] // U
    assert n2 == 4 and n1 == 8
    loads[("og", 0)].wait()
    for k in range(GX):
        loads[("h", "away", 0, k)].wait()
    product(cs, other_c, 0, 4, h_v, True, og_v, 0, pl.ds(0, half))
    loads[("og", 1)].wait()
    for k in range(GX):
        loads[("h", "away", 1, k)].wait()
    product(cs, other_c, 0, 4, h_v, True, og_v, 0, pl.ds(half, half), True)
    send_core(0, 0, 2)
    send_core(1, 2, 2)
    for k in range(GX):
        loads[("h", "home", k)].wait()
    product(hv, c, 0, 4, h_v, True, og_v, 0)
    chip_landed(0, 0, 2)
    step_chip(0)
    loads["w2"].wait()
    back(every, 0, 4)
    chip_landed(1, 2, 2)
    step_chip(1)
    loads["x"].wait()
    away_two(2, 4, x_v, dh_v, 0)
    slots_line()
    product(hv, c, 4, 4, x_v, False, dh_v, 0)
    chip_landed(2, 4, 2)
    step_chip(2)
    step_first(0)
    back(every, 4, 4)
    chip_landed(3, 6, 2)
    step_chip(3)
    step_first(1)
    away_two(4, 8, x_v, dh_v, 4)
    product(hv, c, 8, 4, x_v, False, dh_v, 4)
    chip_landed(4, 8, 2)
    step_chip(4)
    step_second(0)
    step_first(2)
    chip_landed(5, 10, 2)
    step_chip(5)
    step_chip(6)
    step_second(1)
    slots_here(0)
    table_tiles(0, 0, 4 * some)
    step_first(3)
    step_second(2)
    slots_core()
    loads["tab"].wait()
    loads["st"].wait()
    step_first(4)
    slots_here(1)
    table_tiles(1, 0, some)
    step_first(5)
    step_second(3)
    table_tiles(1, some, 2 * some)
    step_first(6)
    step_second(4)
    table_tiles(1, 2 * some, 3 * some)
    step_second(5)
    table_tiles(1, 3 * some, tiles)
    step_second(6)
    for j in range(7):
        step_line(j)
    for i in range(3):
        left_here(ij.at[0], 2 * i)
        left_here(sb.at[:, 0, 0], 2 * i + 1)
    left_here(iz.at[rest], 12)
    left_here(eb.at[rest], 13)
    left_here(iz.at[0], 14)
    left_here(eb.at[0], 15)
    left_here(iz.at[rest], 16)
    left_here(eb.at[rest], 17)
    left_here(cs, 8)
    left_here(xs, 9)
    left_here(ys, 10)
    left_here(zs.at[pl.ds(1, DH - 1)], 11)


def store(*refs):
    ins, outs, sems = refs[:4], refs[4:8], refs[8]
    copies = [pltpu.make_async_copy(a, b, sems.at[i]) for i, (a, b) in enumerate(zip(ins, outs))]
    for copy in copies:
        copy.start()
    for copy in copies:
        copy.wait()


def solution(mesh):
    G, D = mesh.shape["grp"], mesh.shape["dev"]

    def on_device(
        layer_input, hidden_pre, out_grad, second_weight,
        row_grads, row_ids, block_counts, emb_table, adagrad_state,
    ):
        T, IN = layer_input.shape
        HID, OUT = second_weight.shape
        E = row_grads.shape[1]
        cap = row_grads.shape[0] // D
        assert LANES // cap == 2
        GX, DH = G // 2, D // 2
        R1, R2 = IN // (G * D), HID // (G * D)
        assert R1 == R2
        U = LANES
        N = (OUT + HID) // U
        hbm = pl.BlockSpec(memory_space=pltpu.HBM)
        vmem = pl.BlockSpec(memory_space=pltpu.VMEM)
        dma = pltpu.SemaphoreType.DMA
        operands = (
            layer_input, hidden_pre, out_grad, second_weight,
            row_grads.reshape(DH, 2, cap, E), row_ids.reshape(DH, LANES), block_counts,
            emb_table, adagrad_state,
        )
        grads = pl.pallas_call(
            functools.partial(kernel, G, D),
            out_shape=[
                jax.ShapeDtypeStruct((R1, HID), f32),
                jax.ShapeDtypeStruct((R2, OUT), f32),
                jax.ShapeDtypeStruct(emb_table.shape, f32),
                jax.ShapeDtypeStruct(adagrad_state.shape, f32),
            ],
            in_specs=[hbm] * 9,
            out_specs=[vmem] * 4,
            scratch_shapes=[
                pltpu.VMEM((T, IN), bf16),
                pltpu.VMEM((T, HID), bf16),
                pltpu.VMEM((T, OUT), bf16),
                pltpu.VMEM((HID, OUT), bf16),
                pltpu.VMEM((T, HID), bf16),
                pltpu.VMEM((DH, LANES), jnp.int32),
                pltpu.SMEM((D,), jnp.int32),
                pltpu.VMEM((N, GX, D * R1, U), f32),
                pltpu.VMEM((N, GX, D * R1, U), f32),
                pltpu.VMEM((N, GX, D * R1, U), f32),
                pltpu.VMEM((N, 2, DH, R1, U), bf16),
                pltpu.VMEM((N, 2, DH, R1, U), bf16),
                pltpu.VMEM((N, DH, R1, U), bf16),
                pltpu.VMEM((N, DH, R1, U), bf16),
                pltpu.VMEM((N, DH, R1, U), f32),
                pltpu.VMEM((DH, N, R1, U), bf16),
                pltpu.VMEM((DH, N, R1, U), bf16),
                pltpu.VMEM((DH, GX, 2, cap, E), bf16),
                pltpu.VMEM((DH, GX, 2, cap, E), bf16),
                pltpu.VMEM((DH, GX, 2, cap, E), bf16),
                pltpu.VMEM((2, DH, 1, LANES), jnp.int32),
                pltpu.VMEM((DH, GX, 2, 1, LANES), jnp.int32),
                pltpu.VMEM((DH, GX, 2, 1, LANES), jnp.int32),
                pltpu.VMEM((DH, GX, 2, 1, LANES), jnp.int32),
                pltpu.VMEM(emb_table.shape, f32),
                dma((15,)),
                dma((18,)),
                dma((6,)), dma((7,)), dma((7,)), dma((7,)),
                dma((12,)),
            ],
            compiler_params=pltpu.CompilerParams(
                collective_id=0, has_side_effects=True, vmem_limit_bytes=48 * 1024 * 1024
            ),
        )(*[pltpu.with_memory_space_constraint(a, pltpu.HBM) for a in operands])
        return pl.pallas_call(
            store,
            out_shape=[jax.ShapeDtypeStruct(a.shape, a.dtype) for a in grads],
            in_specs=[vmem] * 4,
            out_specs=[hbm] * 4,
            scratch_shapes=[dma((4,))],
            compiler_params=pltpu.CompilerParams(vmem_limit_bytes=8 * 1024 * 1024),
        )(*grads)

    return jax.shard_map(
        on_device,
        mesh=mesh,
        in_specs=(
            P(("grp", "dev"), None),
            P(("grp", "dev"), None),
            P(("grp", "dev"), None),
            P(),
            P(("grp", "dev"), None),
            P(("grp", "dev")),
            P(("grp", "dev")),
            P("dev", None),
            P("dev", None),
        ),
        out_specs=(P(("grp", "dev"), None), P(("grp", "dev"), None), P("dev", None), P("dev", None)),
        check_vma=False,
    )
```

time: 44.1 us -> 34.1 us (0.77)
  local copies, waits for them, and re-layouts: 6.75 us -> 0 us
  Pallas kernels: 36.4 us -> 33.2 us
    unnamed x10 -> x0, local copies, waits for them, and re-layouts: 6.75 us -> none
    pallas_call x1 -> x2, Pallas kernels: 36.4 us -> 33.2 us  [the longest x1 31.8 us: on_device(): pl.pallas_call(functools.partial(kernel, G, D), out_shape=[jax.ShapeDtype...]
where the time goes in v2:
time: 34.1 us; the launch traced here: 33.9 us
  Pallas kernels  33.2 us (97%)
  between operations  0.64 us (2%)
    pallas_call x1, Pallas kernels, on_device(): pl.pallas_call(functools.partial(kernel, G, D), out_shape=[jax.ShapeDtype...  31.8 us
    pallas_call x1, Pallas kernels, on_device(): pl.pallas_call(store, out_shape=[jax.ShapeDtypeStruct(a.shape, a.dtype) f...  1.42 us

profile of v2, /device:TPU:0, one launch (start us, length us, event | category | flops | bytes accessed | tf_op | source)
XLA Modules:
  0.0 33.9 jit_solution(3650900707051905187)
XLA Ops:
  0.6 31.8 %shard_map.120 = (f32[32,1024]{1,0:T(8,128)S(1)}, f32[32,512]{1,0:T(8,128)S(1)}, f32[2048,128]{1,0:T(8,128)S(1)}, f32[2048,128]{1,0:T(8,128)S(1)}) custom-call(bf16[2048,1024]{1,0:T(8,128)(2,1)} %x_hbm.1, bf16[2048,1024]{1,0:T(8,128)(2,1)} %h_hbm.1, bf16[2048,512]{1,0:T(8,128)(2,1)} %og_hbm.1, bf16[1024,512]{1,0:T(8,128)(2,1)} %w2_hbm.1, ...), custom_call_target="tpu_custom_call" | custom-call | tf_op jit(solution)/shard_map/pallas_call | solution.py:383
  32.5 1.4 %shard_map.121 = (f32[32,1024]{1,0:T(8,128)}, f32[32,512]{1,0:T(8,128)}, f32[2048,128]{1,0:T(8,128)}, f32[2048,128]{1,0:T(8,128)}) custom-call(f32[32,1024]{1,0:T(8,128)S(1)} %get-tuple-element.8.refs_0_, f32[32,512]{1,0:T(8,128)S(1)} %get-tuple-element.9.refs_1_, f32[2048,128]{1,0:T(8,128)S(1)} %get-tuple-element.10.refs_2_, ...), custom_call_target="tpu_custom_call" | custom-call | tf_op jit(solution)/shard_map/pallas_call | solution.py:428

commit v3 on v2

--- a/solution.py
+++ b/solution.py
@@ -19,9 +19,9 @@
     x_hbm, h_hbm, og_hbm, w2_hbm, rg_hbm, ids_hbm, cnt_hbm, tab_hbm, st_hbm,
     g1_ref, g2_ref, tab_ref, st_ref,
     x_v, h_v, og_v, w2_v, dh_v, ids_v, cnt_s,
-    hv, cs, cr, xs, xr, ys, yr, fv, zs, zr,
+    hv, cs, cr, xs, xr, ys, yr, fv, zs, zr, ds, dr, zx, zy, fz, px, py,
     sb, eb, eo, ij, iw, iz, io,
-    sums, lsem, s_sem, c_sem, x_sem, y_sem, z_sem, e_sem,
+    sums, lsem, s_sem, c_sem, x_sem, y_sem, z_sem, e_sem, d_sem,
 ):
     GX, DH = G // 2, D // 2
     assert GX == 2
@@ -175,7 +175,9 @@
         rows = pl.ds(pl.multiple_of((b * 2 + pick(q, p)) * R, R), R)
         return hv[n, k, rows, :] + cr[n, k, rows, :]
 
-    pieces = [(0, 2), (2, 2), (4, 2), (6, 2), (8, 2), (10, 1), (11, 1)]
+    pieces = [(0, 2), (2, 2), (4, 2), (6, 2), (8, 1), (9, 1), (10, 1), (11, 1)]
+    late, over_z = 6, [7]
+    units = [sum(w for j, (_, w) in enumerate(pieces) if j not in skip) for skip in (over_z + [late], over_z)]
 
     def chip_landed(j, n, w):
         landed(cr.at[pl.ds(n, w)], c_sem.at[j])
@@ -200,6 +202,68 @@
         for u in range(n, n + w):
             for b in range(DH):
                 fv[u, b] = chip_sum(u, p_me, q_me, b) + xr[u, q_me, b].astype(f32)
+
+    def step_plane(j):
+        n, w = pieces[j]
+        for i, (p, q, to) in enumerate(
+            ((p_no, q_no, diagonal), (p_no, q_me, first_peer), (p_me, q_no, second_peer))
+        ):
+            for u in range(w):
+                for b in range(DH):
+                    ds[i, j - late, u, b] = chip_sum(n + u, p, q, b).astype(bf16)
+            send(ds.at[i, j - late], dr.at[i, j - late], 18, d_sem.at[i, j - late], to)
+
+    def plane_landed(j):
+        n, w = pieces[j]
+        for i in range(1, 4):
+            landed(dr.at[i % 3, j - late], d_sem.at[i % 3, j - late])
+        for b in range(DH):
+            for u in range(w):
+                value = chip_sum(n + u, p_me, q_me, b)
+                for i in range(3):
+                    value = value + dr[i, j - late, u, b].astype(f32)
+                zs[b, n + u] = value.astype(bf16)
+                fv[n + u, b] = value
+        for k, pd in line[::-1]:
+            at = pl.ds(n, w)
+            send(zs.at[(dh + k) % DH, at], zr.at[k, at], 11, z_sem.at[j], (g, pd))
+
+    def line_first(j):
+        n, _ = pieces[j]
+        o = over_z.index(j)
+        for b in range(DH):
+            for p in range(2):
+                for q in range(2):
+                    zx[o, b, p, q] = chip_sum(n, p, q, b).astype(bf16)
+        for k, pd in line[::-1]:
+            send(zx.at[o, (dh + k) % DH], zy.at[o, k], 19, z_sem.at[j], (g, pd))
+
+    def line_plane(j):
+        n, _ = pieces[j]
+        o = over_z.index(j)
+        landed(zy.at[o, pl.ds(1, DH - 1)], z_sem.at[j])
+
+        def line_sum(p, q):
+            value = chip_sum(n, p, q, dh)
+            for k, pd in line:
+                value = value + zy[o, k, p, q].astype(f32)
+            return value
+
+        for i, (p, q, to) in enumerate(
+            ((p_no, q_no, diagonal), (p_no, q_me, first_peer), (p_me, q_no, second_peer))
+        ):
+            px[o, i] = line_sum(p, q).astype(bf16)
+            send(px.at[o, i], py.at[o, i], 20, d_sem.at[i, 1 + o], to)
+        fz[o] = line_sum(p_me, q_me)
+
+    def line_end(j):
+        n, _ = pieces[j]
+        o = over_z.index(j)
+        value = fz[o]
+        for i in range(3):
+            landed(py.at[o, i], d_sem.at[i, 1 + o])
+            value = value + py[o, i].astype(f32)
+        g1_ref[:, (n - n2) * U : (n - n2 + 1) * U] = value
 
     def step_second(j):
         n, w = pieces[j]
@@ -304,33 +368,33 @@
     product(hv, c, 8, 4, x_v, False, dh_v, 4)
     chip_landed(4, 8, 2)
     step_chip(4)
+    step_chip(5)
+    chip_landed(5, 10, 2)
+    step_plane(6)
+    line_first(7)
+    step_first(2)
     step_second(0)
-    step_first(2)
-    chip_landed(5, 10, 2)
-    step_chip(5)
-    step_chip(6)
     step_second(1)
     slots_here(0)
-    table_tiles(0, 0, 4 * some)
+    table_tiles(0, 0, 2 * some)
     step_first(3)
+    table_tiles(0, 2 * some, 4 * some)
+    slots_core()
+    step_first(4)
+    step_first(5)
     step_second(2)
-    slots_core()
     loads["tab"].wait()
     loads["st"].wait()
-    step_first(4)
+    step_second(3)
+    plane_landed(6)
+    step_second(4)
+    line_plane(7)
+    step_second(5)
     slots_here(1)
-    table_tiles(1, 0, some)
-    step_first(5)
-    step_second(3)
-    table_tiles(1, some, 2 * some)
-    step_first(6)
-    step_second(4)
-    table_tiles(1, 2 * some, 3 * some)
-    step_second(5)
-    table_tiles(1, 3 * some, tiles)
-    step_second(6)
+    table_tiles(1, 0, tiles)
     for j in range(7):
         step_line(j)
+    line_end(7)
     for i in range(3):
         left_here(ij.at[0], 2 * i)
         left_here(sb.at[:, 0, 0], 2 * i + 1)
@@ -341,9 +405,12 @@
     left_here(iz.at[rest], 16)
     left_here(eb.at[rest], 17)
     left_here(cs, 8)
-    left_here(xs, 9)
-    left_here(ys, 10)
-    left_here(zs.at[pl.ds(1, DH - 1)], 11)
+    left_here(xs.at[pl.ds(0, units[0])], 9)
+    left_here(ys.at[pl.ds(0, units[0])], 10)
+    left_here(ds, 18)
+    left_here(zx.at[:, pl.ds(1, DH - 1)], 19)
+    left_here(px, 20)
+    left_here(zs.at[pl.ds(1, DH - 1), pl.ds(0, units[1])], 11)
 
 
 def store(*refs):
@@ -408,6 +475,13 @@
                 pltpu.VMEM((N, DH, R1, U), f32),
                 pltpu.VMEM((DH, N, R1, U), bf16),
                 pltpu.VMEM((DH, N, R1, U), bf16),
+                pltpu.VMEM((3, 1, 1, DH, R1, U), bf16),
+                pltpu.VMEM((3, 1, 1, DH, R1, U), bf16),
+                pltpu.VMEM((1, DH, 2, 2, R1, U), bf16),
+                pltpu.VMEM((1, DH, 2, 2, R1, U), bf16),
+                pltpu.VMEM((1, R1, U), f32),
+                pltpu.VMEM((1, 3, R1, U), bf16),
+                pltpu.VMEM((1, 3, R1, U), bf16),
                 pltpu.VMEM((DH, GX, 2, cap, E), bf16),
                 pltpu.VMEM((DH, GX, 2, cap, E), bf16),
                 pltpu.VMEM((DH, GX, 2, cap, E), bf16),
@@ -417,9 +491,10 @@
                 pltpu.VMEM((DH, GX, 2, 1, LANES), jnp.int32),
                 pltpu.VMEM(emb_table.shape, f32),
                 dma((15,)),
-                dma((18,)),
-                dma((6,)), dma((7,)), dma((7,)), dma((7,)),
+                dma((21,)),
+                dma((6,)), dma((8,)), dma((8,)), dma((8,)),
                 dma((12,)),
+                dma((3, 1 + 1)),
             ],
             compiler_params=pltpu.CompilerParams(
                 collective_id=0, has_side_effects=True, vmem_limit_bytes=48 * 1024 * 1024

time: 34.1 us -> 33.2 us (0.974)
  Pallas kernels: 33.2 us -> 32.4 us
    pallas_call x1, Pallas kernels: 31.8 us -> 31 us  [on_device(): pl.pallas_call(functools.partial(kernel, G, D), out_shape=[jax.ShapeDtype...]
where the time goes in v3:
time: 33.2 us; the launch traced here: 33.1 us
  Pallas kernels  32.4 us (98%)
  between operations  0.64 us (2%)
    pallas_call x1, Pallas kernels, on_device(): pl.pallas_call(functools.partial(kernel, G, D), out_shape=[jax.ShapeDtype...  31 us
    pallas_call x1, Pallas kernels, on_device(): pl.pallas_call(store, out_shape=[jax.ShapeDtypeStruct(a.shape, a.dtype) f...  1.42 us

profile of v3, /device:TPU:0, one launch (start us, length us, event | category | flops | bytes accessed | tf_op | source)
XLA Modules:
  0.0 33.1 jit_solution(10316799655788559275)
XLA Ops:
  0.6 31.0 %shard_map.120 = (f32[32,1024]{1,0:T(8,128)S(1)}, f32[32,512]{1,0:T(8,128)S(1)}, f32[2048,128]{1,0:T(8,128)S(1)}, f32[2048,128]{1,0:T(8,128)S(1)}) custom-call(bf16[2048,1024]{1,0:T(8,128)(2,1)} %x_hbm.1, bf16[2048,1024]{1,0:T(8,128)(2,1)} %h_hbm.1, bf16[2048,512]{1,0:T(8,128)(2,1)} %og_hbm.1, bf16[1024,512]{1,0:T(8,128)(2,1)} %w2_hbm.1, ...), custom_call_target="tpu_custom_call" | custom-call | tf_op jit(solution)/shard_map/pallas_call | solution.py:450
  31.7 1.4 %shard_map.121 = (f32[32,1024]{1,0:T(8,128)}, f32[32,512]{1,0:T(8,128)}, f32[2048,128]{1,0:T(8,128)}, f32[2048,128]{1,0:T(8,128)}) custom-call(f32[32,1024]{1,0:T(8,128)S(1)} %get-tuple-element.8.refs_0_, f32[32,512]{1,0:T(8,128)S(1)} %get-tuple-element.9.refs_1_, f32[2048,128]{1,0:T(8,128)S(1)} %get-tuple-element.10.refs_2_, ...), custom_call_target="tpu_custom_call" | custom-call | tf_op jit(solution)/shard_map/pallas_call | solution.py:503

commit v4 on v3

--- a/solution.py
+++ b/solution.py
@@ -112,6 +112,10 @@
     for i, (to, y, _, _, moved) in enumerate(plane):
         send(ij.at[moved], iw.at[:, gx, dl], 2 * i, e_sem.at[2 * i], to)
         send(rg_hbm.at[:, y], sb.at[:, gx, dl], 2 * i + 1, e_sem.at[2 * i + 1], to)
+    for k, pd in line[::-1]:
+        t = (dh + k) % DH
+        send(ij.at[0, t], iz.at[k, gx, dl], 12, e_sem.at[6], (g, pd))
+        send(rg_hbm.at[t, dl], eb.at[k, gx, dl], 13, e_sem.at[7], (g, pd))
 
     def slots_line():
         loads["own"].wait()
@@ -120,8 +124,9 @@
             landed(sb.at[:, a, b], e_sem.at[2 * i + 1])
         for k, pd in line[::-1]:
             t = (dh + k) % DH
-            send(iw.at[t], iz.at[k], 12, e_sem.at[6], (g, pd))
-            send(sb.at[t], eb.at[k], 13, e_sem.at[7], (g, pd))
+            for at in ((gx, odl), (ox,)):
+                send(iw.at[(t, *at)], iz.at[(k, *at)], 12, e_sem.at[6], (g, pd))
+                send(sb.at[(t, *at)], eb.at[(k, *at)], 13, e_sem.at[7], (g, pd))
         send(iw.at[dh], io.at[0], 14, e_sem.at[8], core_peer)
         send(sb.at[dh], eo.at[0], 15, e_sem.at[9], core_peer)
 
@@ -167,6 +172,15 @@
 
         lax.fori_loop(0, 2, body, 0)
 
+    def home_two(n, src, rhs, at, after):
+        def body(i, _):
+            product(hv, c, n + 2 * i, 2, src, False, rhs, at + 2 * i)
+            for k in range(2):
+                pl.when(i == k)(after[k])
+            return 0
+
+        lax.fori_loop(0, 2, body, 0)
+
     p_me, q_me = pick(gx, dl), pick(dl, gx)
     p_no, q_no = 1 - p_me, 1 - q_me
 
@@ -175,8 +189,8 @@
         rows = pl.ds(pl.multiple_of((b * 2 + pick(q, p)) * R, R), R)
         return hv[n, k, rows, :] + cr[n, k, rows, :]
 
-    pieces = [(0, 2), (2, 2), (4, 2), (6, 2), (8, 1), (9, 1), (10, 1), (11, 1)]
-    late, over_z = 6, [7]
+    pieces = [(0, 2), (2, 1), (4, 2), (6, 2), (8, 1), (9, 1), (10, 1), (11, 1), (3, 1)]
+    late, over_z = 6, [7, 8]
     units = [sum(w for j, (_, w) in enumerate(pieces) if j not in skip) for skip in (over_z + [late], over_z)]
 
     def chip_landed(j, n, w):
@@ -263,7 +277,8 @@
         for i in range(3):
             landed(py.at[o, i], d_sem.at[i, 1 + o])
             value = value + py[o, i].astype(f32)
-        g1_ref[:, (n - n2) * U : (n - n2 + 1) * U] = value
+        out, at = (g2_ref, n) if n < n2 else (g1_ref, n - n2)
+        out[:, at * U : (at + 1) * U] = value
 
     def step_second(j):
         n, w = pieces[j]
@@ -352,6 +367,7 @@
     loads["w2"].wait()
     back(every, 0, 4)
     chip_landed(1, 2, 2)
+    line_first(8)
     step_chip(1)
     loads["x"].wait()
     away_two(2, 4, x_v, dh_v, 0)
@@ -378,6 +394,7 @@
     slots_here(0)
     table_tiles(0, 0, 2 * some)
     step_first(3)
+    line_plane(8)
     table_tiles(0, 2 * some, 4 * some)
     slots_core()
     step_first(4)
@@ -394,6 +411,7 @@
     table_tiles(1, 0, tiles)
     for j in range(7):
         step_line(j)
+    line_end(8)
     line_end(7)
     for i in range(3):
         left_here(ij.at[0], 2 * i)
@@ -415,8 +433,14 @@
 
 def store(*refs):
     ins, outs, sems = refs[:4], refs[4:8], refs[8]
-    copies = [pltpu.make_async_copy(a, b, sems.at[i]) for i, (a, b) in enumerate(zip(ins, outs))]
-    for copy in copies:
+    copies = []
+    for a, b in zip(ins, outs):
+        parts = sems.shape[0] // 4
+        rows = a.shape[0] // parts
+        for i in range(parts):
+            at = pl.ds(i * rows, rows)
+            copies.append(pltpu.make_async_copy(a.at[at], b.at[at], sems.at[len(copies)]))
+    for copy in copies[::-1]:
         copy.start()
     for copy in copies:
         copy.wait()
@@ -477,11 +501,11 @@
                 pltpu.VMEM((DH, N, R1, U), bf16),
                 pltpu.VMEM((3, 1, 1, DH, R1, U), bf16),
                 pltpu.VMEM((3, 1, 1, DH, R1, U), bf16),
-                pltpu.VMEM((1, DH, 2, 2, R1, U), bf16),
-                pltpu.VMEM((1, DH, 2, 2, R1, U), bf16),
-                pltpu.VMEM((1, R1, U), f32),
-                pltpu.VMEM((1, 3, R1, U), bf16),
-                pltpu.VMEM((1, 3, R1, U), bf16),
+                pltpu.VMEM((2, DH, 2, 2, R1, U), bf16),
+                pltpu.VMEM((2, DH, 2, 2, R1, U), bf16),
+                pltpu.VMEM((2, R1, U), f32),
+                pltpu.VMEM((2, 3, R1, U), bf16),
+                pltpu.VMEM((2, 3, R1, U), bf16),
                 pltpu.VMEM((DH, GX, 2, cap, E), bf16),
                 pltpu.VMEM((DH, GX, 2, cap, E), bf16),
                 pltpu.VMEM((DH, GX, 2, cap, E), bf16),
@@ -492,9 +516,9 @@
                 pltpu.VMEM(emb_table.shape, f32),
                 dma((15,)),
                 dma((21,)),
-                dma((6,)), dma((8,)), dma((8,)), dma((8,)),
+                dma((6,)), dma((9,)), dma((9,)), dma((9,)),
                 dma((12,)),
-                dma((3, 1 + 1)),
+                dma((3, 1 + 2)),
             ],
             compiler_params=pltpu.CompilerParams(
                 collective_id=0, has_side_effects=True, vmem_limit_bytes=48 * 1024 * 1024
@@ -505,7 +529,7 @@
             out_shape=[jax.ShapeDtypeStruct(a.shape, a.dtype) for a in grads],
             in_specs=[vmem] * 4,
             out_specs=[hbm] * 4,
-            scratch_shapes=[dma((4,))],
+            scratch_shapes=[dma((4 * 1,))],
             compiler_params=pltpu.CompilerParams(vmem_limit_bytes=8 * 1024 * 1024),
         )(*grads)
 

time: 33.2 us -> 32.8 us (0.988)
  Pallas kernels: 32.4 us -> 32 us
    pallas_call x1, Pallas kernels: 31 us -> 30.6 us  [on_device(): pl.pallas_call(functools.partial(kernel, G, D), out_shape=[jax.ShapeDtype...]
where the time goes in v4:
time: 32.8 us; the launch traced here: 32.6 us
  Pallas kernels  32 us (98%)
  between operations  0.64 us (2%)
    pallas_call x1, Pallas kernels, on_device(): pl.pallas_call(functools.partial(kernel, G, D), out_shape=[jax.ShapeDtype...  30.6 us
    pallas_call x1, Pallas kernels, on_device(): pl.pallas_call(store, out_shape=[jax.ShapeDtypeStruct(a.shape, a.dtype) f...  1.41 us

profile of v4, /device:TPU:0, one launch (start us, length us, event | category | flops | bytes accessed | tf_op | source)
XLA Modules:
  0.0 32.6 jit_solution(4667215194952966120)
XLA Ops:
  0.6 30.6 %shard_map.120 = (f32[32,1024]{1,0:T(8,128)S(1)}, f32[32,512]{1,0:T(8,128)S(1)}, f32[2048,128]{1,0:T(8,128)S(1)}, f32[2048,128]{1,0:T(8,128)S(1)}) custom-call(bf16[2048,1024]{1,0:T(8,128)(2,1)} %x_hbm.1, bf16[2048,1024]{1,0:T(8,128)(2,1)} %h_hbm.1, bf16[2048,512]{1,0:T(8,128)(2,1)} %og_hbm.1, bf16[1024,512]{1,0:T(8,128)(2,1)} %w2_hbm.1, ...), custom_call_target="tpu_custom_call" | custom-call | tf_op jit(solution)/shard_map/pallas_call | solution.py:474
  31.2 1.4 %shard_map.121 = (f32[32,1024]{1,0:T(8,128)}, f32[32,512]{1,0:T(8,128)}, f32[2048,128]{1,0:T(8,128)}, f32[2048,128]{1,0:T(8,128)}) custom-call(f32[32,1024]{1,0:T(8,128)S(1)} %get-tuple-element.8.refs_0_, f32[32,512]{1,0:T(8,128)S(1)} %get-tuple-element.9.refs_1_, f32[2048,128]{1,0:T(8,128)S(1)} %get-tuple-element.10.refs_2_, ...), custom_call_target="tpu_custom_call" | custom-call | tf_op jit(solution)/shard_map/pallas_call | solution.py:527
